TPU v7x, 32 devices: a 4x4x1 block of a 4x4x8 slice. The times are simulated.
32 devices in a mesh: dp: 1 (over z), tp: 4 (over y), ep: 8 (over x, core).
Axes of the slice: x: 4, y: 4, z: 1, core: 2. Of those that a mesh axis runs over, the one named last changes fastest.
The devices are a block of a 4x4x8 slice.
Arguments:
- tokens: bfloat16 [1024, 2048], P(('dp', 'ep', 'tp'))
- expert_ids: int32 [1024, 8], P(('dp', 'ep', 'tp'))
- gates: float32 [1024, 8], P(('dp', 'ep', 'tp'))
- w_gate: bfloat16 [128, 2048, 768], P('ep', None, 'tp')
- w_up: bfloat16 [128, 2048, 768], P('ep', None, 'tp')
- w_down: bfloat16 [128, 768, 2048], P('ep', 'tp')
Outputs:
- output: bfloat16 [1024, 2048], P(('dp', 'ep', 'tp'))
All inputs are finite; a program needn't handle non-finite values.
Results may differ from a plain program's by a relative error of at most 0.0012.
Values are sent between devices in bfloat16 or wider.
A program may use at most 768 MiB of HBM per device.

v0:
```python
import jax
import jax.numpy as jnp
from jax import lax
from jax.sharding import PartitionSpec as P


def solution(mesh):
    ep_size = mesh.shape["ep"]
    row_spec = P(("dp", "ep", "tp"), None)

    def local_layer(tokens, expert_ids, gates, w_gate, w_up, w_down):
        top_k = expert_ids.shape[1]
        local_experts = w_gate.shape[0]
        hidden = tokens.shape[1]
        all_tokens = lax.all_gather(tokens, ("ep", "tp"), tiled=True)
        all_ids = lax.all_gather(expert_ids, ("ep", "tp"), tiled=True)
        all_gates = lax.all_gather(gates, ("ep", "tp"), tiled=True)
        group_rows = all_tokens.shape[0]
        load = group_rows * top_k // (local_experts * ep_size)
        local_ids = all_ids.reshape(-1) - lax.axis_index("ep") * local_experts
        is_mine = (local_ids >= 0) & (local_ids < local_experts)
        sort_key = jnp.where(is_mine, local_ids, local_experts)
        order = jnp.argsort(sort_key, stable=True)[: local_experts * load].reshape(local_experts, load)
        row_index = order // top_k
        gate_disp = all_gates.reshape(-1)[order]
        x_disp = all_tokens[row_index]
        hidden_gate = jnp.einsum("ecd,edf->ecf", x_disp, w_gate, preferred_element_type=jnp.float32)
        hidden_up = jnp.einsum("ecd,edf->ecf", x_disp, w_up, preferred_element_type=jnp.float32)
        act_rows = (jax.nn.silu(hidden_gate) * hidden_up).astype(jnp.bfloat16)
        out_rows = jnp.einsum("ecf,efd->ecd", act_rows, w_down, preferred_element_type=jnp.float32)
        weighted = (out_rows * gate_disp[:, :, None]).reshape(-1, hidden)
        partial_sum = jax.ops.segment_sum(weighted, row_index.reshape(-1), num_segments=group_rows)
        own_rows = lax.psum_scatter(partial_sum, ("ep", "tp"), scatter_dimension=0, tiled=True)
        return own_rows.astype(jnp.bfloat16)

    return jax.shard_map(local_layer, mesh=mesh, in_specs=(row_spec, row_spec, row_spec, P("ep", None, "tp"), P("ep", None, "tp"), P("ep", "tp", None)), out_specs=row_spec, check_vma=False)
```

profile of v0, /device:TPU:97, one launch (start us, length us, event | category | flops | bytes accessed | tf_op | source)
XLA Modules:
  0.0 238.3 jit_solution(1925315683100546668)
XLA Ops:
  6.5 0.0 all-gather.4.cloned.1.call-start
  6.6 0.7 all-gather.4.cloned.1.call-update
  7.3 0.1 reduce-scatter.2.cloned.1.call-start
  7.4 32.5 %all-gather.1 = f32[32,32,8]{1,2,0:T(8,128)S(1)} all-gather(f32[1,32,8]{1,2,0:T(8,128)} %bitcast.12), channel_id=1, replica_groups=mesh['dp'=1,'tp'=4,'ep'=8] {'ep','tp'}, dimensions={0}, use_global_device_ids=true | all-gather | bytes 33792 | tf_op jit(solution)/shard_map/all_gather | solution.py:17
  39.9 0.2 copy.10
  40.1 0.3 reshape.19
  40.4 33.0 %all-gather = s32[32,32,8]{1,2,0:T(8,128)S(1)} all-gather(s32[1,32,8]{1,2,0:T(8,128)} %bitcast.13), channel_id=1, replica_groups=mesh['dp'=1,'tp'=4,'ep'=8] {'ep','tp'}, dimensions={0}, use_global_device_ids=true | all-gather | bytes 33792 | tf_op jit(solution)/shard_map/all_gather | solution.py:16
  73.4 0.2 copy.9
  73.6 0.3 sub.17
  73.9 6.8 %sort.17 = (s32[8192]{0:T(1024)}, s32[8192]{0:T(1024)S(1)}) sort(s32[8192]{0:T(1024)S(1)} %and_select_fusion, s32[8192]{0:T(1024)S(1)} %iota.4), dimensions={0}, to_apply=%region_0.1 | sort | flops 106496 | bytes 131072 | tf_op jit(solution)/shard_map/jit(argsort)/sort | solution.py:23
  80.7 0.1 slice.14
  80.8 0.1 reshape.23
  80.8 0.1 reshape.31
  80.9 6.3 %gather_fusion.1 = f32[1024]{0:T(1024)S(1)} fusion(f32[8192]{0:T(1024)S(1)} %reshape.19, s32[1024]{0:T(1024)S(1)} %broadcast_clamp_fusion), kind=kCustom, calls=%fused_computation.1 | custom fusion | bytes 12288 | tf_op jit(solution)/shard_map/gather | solution.py:25
  87.2 0.1 reshape.30
  87.2 0.1 reshape.39
  87.3 0.0 all-gather.4.cloned.1.call-done
  87.3 11.6 %gather_fusion = bf16[1024,2048]{1,0:T(8,128)(2,1)} fusion(bf16[1024,2048]{1,0:T(8,128)(2,1)} %all-gather.4.cloned.1.call-done, s32[1024]{0:T(1024)S(1)} %broadcast_clamp_fusion.1), kind=kCustom, calls=%fused_computation | custom fusion | bytes 8392704 | tf_op jit(solution)/shard_map/gather | solution.py:26
  98.9 10.0 %fusion.12 = f32[16,64,192]{2,1,0:T(8,128)S(1)} fusion(bf16[16,64,2048]{2,1,0:T(8,128)(2,1)} %bitcast.9, bf16[16,2048,192]{1,2,0:T(8,128)(2,1)} %param.9), kind=kOutput, calls=%fused_computation.28 | convolution fusion | flops 805306368 | bytes 17563648 | tf_op jit(solution)/shard_map/ecd,edf->ecf/dot_general | solution.py:27
  108.8 14.7 %convolution_multiply_fusion = f32[16,64,2048]{2,1,0:T(8,128)} fusion(bf16[16,192,2048]{2,1,0:T(8,128)(2,1)} %param.11, f32[16,64]{1,0:T(8,128)S(1)} %reshape.30, bf16[16,64,2048]{2,1,0:T(8,128)(2,1)} %bitcast.10, bf16[16,2048,192]{1,2,0:T(8,128)(2,1)} %param.10, f32[16,64,192]{2,1,0:T(8,128)S(1)} %fusion.12), kind=kOutput, calls=%fused_computation.3 | convolution fusion | flops 1613889536 | bytes 38539264 | tf_op jit(solution)/shard_map/ecf,efd->ecd/dot_general | solution.py:30
  123.5 18.6 %scatter_custom_fusion = f32[1024,2048]{1,0:T(8,128)} fusion(s32[1024]{0:T(1024)S(1)} %reshape.39, f32[1024,2048]{1,0:T(8,128)} %bitcast.11, f32[]{:T(128)} %constant.11.clone.1), kind=kCustom, calls=%fused_computation.4 | custom fusion | flops 2097152 | bytes 8389120 | tf_op jit(solution)/shard_map/scatter-add | solution.py:32
  142.1 0.1 reduce-scatter.2.cloned.1.call-update
  142.2 87.7 %reduce-scatter.2.cloned.1.call-done = f32[32,2048]{1,0:T(8,128)} async-done(((f32[1024,2048]{1,0:T(8,128)}), f32[32,2048]{1,0:T(8,128)}) %reduce-scatter.2.cloned.1.call-update) | async-done | bytes 262160 | tf_op jit(solution)/shard_map/reduce_scatter | solution.py:33
  229.9 1.6 convert_element_type.7
  (7 shorter events, 0.1 us)
Async XLA Ops:
  6.5 80.8 %all-gather.4.cloned.1.call-start = ((), (), s32[]{:S(2)}) async-start(), calls=%async_computation.1 | async-start | bytes 4325376 | tf_op jit(solution)/shard_map/all_gather | solution.py:15
  7.3 222.6 %reduce-scatter.2.cloned.1.call-start = ((), (), s32[]{:S(2)}) async-start(), calls=%async_computation.2 | async-start | bytes 8650752 | tf_op jit(solution)/shard_map/reduce_scatter | solution.py:33
Sparse Core Ops, SparseCore 0:
  9.4 45.1 all-gather.3
  142.3 87.5 reduce-scatter.1
where the time goes:
time: 239 us; the launch traced here: 238 us
  waiting for transfers between devices  88.5 us (37%)
  blocking collectives  65.5 us (27%)
  other arithmetic  27 us (11%)
  matrix products  24.6 us (10%)
  local copies, waits for them, and re-layouts  19.1 us (8%)
  between operations  13.5 us (6%)
    reduce_scatter x1, waiting for transfers between devices, local_layer(): lax.psum_scatter(partial_sum, ('ep', 'tp'), scatter_dimension=0, tiled=True)  87.7 us
    all_gather x1, blocking collectives, local_layer(): all_ids = lax.all_gather(expert_ids, ('ep', 'tp'), tiled=True)  33 us
    all_gather x1, blocking collectives, local_layer(): all_gates = lax.all_gather(gates, ('ep', 'tp'), tiled=True)  32.5 us
    scatter-add x1, other arithmetic, local_layer(): jax.ops.segment_sum(weighted, row_index.reshape(-1), num_segments=group_r...  18.6 us
    dot_general x1, matrix products, local_layer(): jnp.einsum('ecf,efd->ecd', act_rows, w_down, preferred_element_type=jnp.f...  14.7 us
    gather x1, local copies, waits for them, and re-layouts, local_layer(): x_disp = all_tokens[row_index]  11.6 us
    dot_general x1, matrix products, local_layer(): jnp.einsum('ecd,edf->ecf', x_disp, w_gate, preferred_element_type=jnp.flo...  9.97 us
    sort x1, other arithmetic, local_layer(): jnp.argsort(sort_key, stable=True)[:local_experts * load]  6.77 us
  transfers between devices with their start and end apart: 2, of which 1 were waited for; matrix products, arithmetic and copies ran while one was open for 6% of the time, Pallas kernels for 0%

commit v1 on v0

v1 whole, which is shorter than its diff:
```python
import functools

import jax
import jax.numpy as jnp
from jax import lax
from jax.experimental import pallas as pl
from jax.experimental.pallas import tpu as pltpu
from jax.sharding import PartitionSpec as P

MESH = pl.DeviceIdType.MESH
BF = jnp.bfloat16
F32 = jnp.float32
CW = 256
WD_SLOTS = 4


def kernel(dims, tok, ids, gat, wg, wu, wd, out,
           xg, meta_src, meta, pmat, xs, wbuf, acc, h_t, lecol, gcol, hexp, wdbuf,
           part, d2d, mrec, nrec,
           ag_send, ag_recv, meta_send, meta_recv, w_sem, wd_sem, rs_send, rs_recv):
    nx, ny, ne, ff, rows, hid = dims
    nch = hid // CW
    group = 2 * nx * ny * rows
    plane = group // 2
    line = ny * rows
    load = group // ne
    ep_n = 2 * nx
    y = lax.axis_index("tp")
    ep = lax.axis_index("ep")
    x = ep // 2
    c = ep % 2
    o = 1 - c

    def dev(xx, yy, cc):
        return {"tp": yy, "ep": 2 * xx + cc}

    def xo(s):
        return lax.rem(x + (s + nx), nx)

    def yo(s):
        return lax.rem(y + (s + ny), ny)

    def w_copy(k, which):
        src = (wg, wu)[which]
        return pltpu.make_async_copy(src.at[:, :, pl.ds(k * CW, CW)],
                                     wbuf.at[k, :, pl.ds(which * ff, ff), :], w_sem.at[k, which])

    def wd_copy(j):
        return pltpu.make_async_copy(wd.at[:, pl.ds(j * CW, CW)], wdbuf.at[j % WD_SLOTS], wd_sem.at[j % WD_SLOTS])

    barrier = pltpu.get_barrier_semaphore()
    n_dev = ep_n * ny
    me = y * ep_n + ep

    def greet(i, carry):
        flat = lax.rem(me + i, n_dev)
        pl.semaphore_signal(barrier, inc=1, device_id={"tp": flat // ep_n, "ep": lax.rem(flat, ep_n)},
                            device_id_type=MESH)
        return carry

    lax.fori_loop(1, n_dev, greet, 0)

    for k in range(nch):
        for which in range(2):
            w_copy(k, which).start()
    for j in range(WD_SLOTS):
        wd_copy(j).start()

    ids4 = jnp.concatenate([ids[...]] * ny, axis=1)
    gat4 = jnp.concatenate([gat[...]] * ny, axis=1)
    lane = lax.broadcasted_iota(jnp.int32, (1, line), 1)
    mine = (lane // rows) == y
    for p in range(ep_n):
        sel = (ids4 // ne) == p
        le = jnp.sum(jnp.where(sel, ids4 - p * ne, 0).astype(F32), axis=0, keepdims=True)
        ga = jnp.sum(jnp.where(sel, gat4, 0.0), axis=0, keepdims=True)
        meta_src[p, :, pl.ds(0, line)] = jnp.where(mine, le, 0.0)
        meta_src[p, :, pl.ds(line, line)] = jnp.where(mine, ga, 0.0)
    my_block = (c * nx + x) * ny + y
    meta[my_block] = meta_src[ep]
    for k in range(nch):
        xg[k, c, x, y] = tok[:, pl.ds(k * CW, CW)]

    pl.semaphore_wait(barrier, n_dev - 1)

    def send_meta(i, carry):
        flat = lax.rem(me + i, n_dev)
        pe = lax.rem(flat, ep_n)
        pltpu.make_async_remote_copy(
            src_ref=meta_src.at[pe], dst_ref=meta.at[my_block], send_sem=meta_send, recv_sem=meta_recv,
            device_id={"tp": flat // ep_n, "ep": pe}, device_id_type=MESH).start()
        return carry

    lax.fori_loop(1, n_dev, send_meta, 0)

    def rcopy(k, kind, src, dst, to):
        return pltpu.make_async_remote_copy(src_ref=src, dst_ref=dst, send_sem=ag_send.at[k, kind],
                                            recv_sem=ag_recv.at[k, kind], device_id=to, device_id_type=MESH)

    def along(k, first, s):
        use_x = (k % 2 == 0) == first
        return dev(xo(s), y, c) if use_x else dev(x, yo(s), c)

    def block(k, s):
        return xg.at[k, c, xo(s), y] if k % 2 == 0 else xg.at[k, c, x, yo(s)]

    def lines(k, s, cc):
        return xg.at[k, cc, :, yo(s)] if k % 2 == 0 else xg.at[k, cc, xo(s)]

    def dirn(k):
        return 1 if (k // 2) % 2 == 0 else -1

    partner = dev(x, y, o)

    def a0(k):
        src = tok.at[:, pl.ds(k * CW, CW)]
        rcopy(k, 0, src, block(k, 0), along(k, True, 1)).start()
        rcopy(k, 1, src, block(k, 0), along(k, True, -1)).start()

    def wait(k, kind, dst):
        rcopy(k, kind, dst, dst, partner).wait_recv()

    def a1(k):
        d = dirn(k)
        first, second = (0, 1) if d == 1 else (1, 0)
        wait(k, first, block(k, -d))
        rcopy(k, 2, block(k, -d), block(k, -d), along(k, True, d)).start()
        wait(k, second, block(k, d))

    def a2(k):
        wait(k, 2, block(k, 2))
        rcopy(k, 3, lines(k, 0, c), lines(k, 0, c), along(k, False, 1)).start()
        rcopy(k, 4, lines(k, 0, c), lines(k, 0, c), along(k, False, -1)).start()
        rcopy(k, 6, lines(k, 0, c), lines(k, 0, c), partner).start()

    def a3(k):
        d = dirn(k)
        first, second = (3, 4) if d == 1 else (4, 3)
        wait(k, first, lines(k, -d, c))
        rcopy(k, 5, lines(k, -d, c), lines(k, -d, c), along(k, False, d)).start()
        rcopy(k, 7, lines(k, -d, c), lines(k, -d, c), partner).start()
        wait(k, second, lines(k, d, c))
        rcopy(k, 8, lines(k, d, c), lines(k, d, c), partner).start()

    def a4(k):
        wait(k, 5, lines(k, 2, c))
        rcopy(k, 9, lines(k, 2, c), lines(k, 2, c), partner).start()

    def a5(k):
        d = dirn(k)
        wait(k, 6, lines(k, 0, o))
        wait(k, 7, lines(k, -d, o))
        wait(k, 8, lines(k, d, o))
        wait(k, 9, lines(k, 2, o))

    n_grp = 2 * nx

    def build_perm():
        all_meta = meta.at[pl.ds(0, n_dev - 1)]
        pltpu.make_async_remote_copy(src_ref=all_meta, dst_ref=all_meta, send_sem=meta_send, recv_sem=meta_recv,
                                     device_id=partner, device_id_type=MESH).wait()
        les, gas = [], []
        for g in range(n_grp):
            row = meta[g * ny]
            for i in range(1, ny):
                row = row + meta[g * ny + i]
            les.append(row[:, :line])
            gas.append(row[:, line:])
        e_iota = lax.broadcasted_iota(jnp.int32, (ne, line), 0).astype(F32)
        hots = [jnp.where(e_iota == le, 1.0, 0.0) for le in les]
        r_i = lax.broadcasted_iota(jnp.int32, (line, line), 0)
        c_i = lax.broadcasted_iota(jnp.int32, (line, line), 1)
        upper = jnp.where(r_i < c_i, 1.0, 0.0).astype(BF)
        before = jnp.dot(jnp.concatenate(hots, axis=0).astype(BF), upper, preferred_element_type=F32)
        off = jnp.zeros((ne, 1), F32)
        s_iota = lax.broadcasted_iota(jnp.int32, (group, line), 0).astype(F32)
        for g in range(n_grp):
            pos = jnp.sum(hots[g] * (e_iota * load + off + before[g * ne:(g + 1) * ne]), axis=0, keepdims=True)
            off = off + jnp.sum(hots[g], axis=1, keepdims=True)
            pmat[:, pl.ds(g * line, line)] = jnp.where(s_iota == pos, 1.0, 0.0).astype(BF)
        le_t = jnp.concatenate(les, axis=0).T
        ga_t = jnp.concatenate(gas, axis=0).T
        for g in range(n_grp):
            lecol[pl.ds(g * line, line), :] = jnp.broadcast_to(le_t[:, g:g + 1], (line, 128))
            gcol[pl.ds(g * line, line), :] = jnp.broadcast_to(ga_t[:, g:g + 1], (line, 128))

    half_lane = lax.broadcasted_iota(jnp.int32, (2 * ff, 2 * load), 1) < load

    def compute(k):
        xk = xg.at[k].reshape(group, CW)

        def perm(m, carry):
            sl = pl.ds(pl.multiple_of(m * (group // 2), group // 2), group // 2)
            xs[sl, :] = jnp.dot(pmat[sl, :], xk[...], preferred_element_type=F32).astype(BF)
            return carry

        lax.fori_loop(0, 2, perm, 0)
        w_copy(k, 0).wait()
        w_copy(k, 1).wait()

        def pair(p, carry):
            rhs = xs[pl.ds(pl.multiple_of(p * 2 * load, 2 * load), 2 * load), :]
            dn = (((1,), (1,)), ((), ()))
            r0 = lax.dot_general(wbuf[k, 2 * p], rhs, dn, preferred_element_type=F32)
            r1 = lax.dot_general(wbuf[k, 2 * p + 1], rhs, dn, preferred_element_type=F32)
            r = jnp.where(half_lane, r0, r1)
            if k == 0:
                acc[p] = r
            else:
                acc[p] = acc[p] + r
            return carry

        lax.fori_loop(0, ne // 2, pair, 0)

    for k in range(nch):
        a0(k)
    lag = 5
    for t in range(nch + lag):
        if t < nch:
            a1(t)
        if 0 <= t - 1 < nch:
            a2(t - 1)
        if 0 <= t - 2 < nch:
            a3(t - 2)
        if 0 <= t - 3 < nch:
            a4(t - 3)
        if t == 3:
            build_perm()
        if 0 <= t - 5 < nch:
            a5(t - 5)
            compute(t - 5)

    for p in range(ne // 2):
        a = acc[p, :ff, :]
        b = acc[p, ff:, :]
        h_t[:, pl.ds(p * 2 * load, 2 * load)] = (jax.nn.silu(a) * b).astype(BF)
    wide = 4 * ff
    col_e = (lax.broadcasted_iota(jnp.int32, (line, wide), 1) // ff).astype(F32)

    def expand(g, carry):
        sl = pl.ds(pl.multiple_of(g * line, line), line)
        ht = jnp.dot(h_t[...], pmat[:, sl], preferred_element_type=F32)
        h = ht.T
        rep = jnp.concatenate([h] * 4, axis=1)
        le = jnp.broadcast_to(lecol[sl, :][:, :1], (line, wide))
        for q in range(ne // 4):
            hexp[sl, pl.ds(q * wide, wide)] = jnp.where(col_e + 4.0 * q == le, rep, 0.0).astype(BF)
        return carry

    lax.fori_loop(0, n_grp, expand, 0)

    def scopy(j, kind, src, dst, to):
        return pltpu.make_async_remote_copy(src_ref=src, dst_ref=dst, send_sem=rs_send.at[j, kind],
                                            recv_sem=rs_recv.at[j, kind], device_id=to, device_id_type=MESH)

    def down(j):
        slot = lax.rem(j, WD_SLOTS)
        pltpu.make_async_copy(wd.at[:, pl.ds(0, CW)], wdbuf.at[slot], wd_sem.at[slot]).wait()

        def one(i, carry):
            cc = jnp.where(i == 0, o, c)
            base = pl.multiple_of(cc * plane, plane)
            v = jnp.dot(hexp[pl.ds(base, plane), :], wdbuf[slot], preferred_element_type=F32)
            gt = gcol[pl.ds(base, plane), :]
            v = jnp.concatenate([v[:, q * 128:(q + 1) * 128] * gt for q in range(CW // 128)], axis=1)
            part[j, cc] = v.reshape(nx, ny, rows, CW)

            @pl.when(i == 0)
            def _():
                scopy(j, 0, part.at[j, o], d2d.at[j], partner).start()

            return carry

        lax.fori_loop(0, 2, one, 0)

        @pl.when(j + WD_SLOTS < nch)
        def _():
            pltpu.make_async_copy(wd.at[:, pl.ds(pl.multiple_of((j + WD_SLOTS) * CW, CW), CW)],
                                  wdbuf.at[slot], wd_sem.at[slot]).start()

    def stages(i, hf):
        j = 2 * i + hf
        d = 1 - 2 * lax.rem(i, 2)

        def xd(s):
            return lax.rem(x + s + 2 * nx, nx)

        def yd(s):
            return lax.rem(y + s + 2 * ny, ny)

        def big(s):
            return part.at[j, c, :, yd(s)] if hf == 0 else part.at[j, c, xd(s)]

        def big_to(s):
            return dev(x, yd(s), c) if hf == 0 else dev(xd(s), y, c)

        def small(s):
            return part.at[j, c, xd(s), y] if hf == 0 else part.at[j, c, x, yd(s)]

        def small_to(s):
            return dev(xd(s), y, c) if hf == 0 else dev(x, yd(s), c)

        def s1():
            scopy(j, 0, d2d.at[j], d2d.at[j], partner).wait_recv()
            part[j, c] = part[j, c] + d2d[j]
            scopy(j, 1, big(2), mrec.at[j, 0], big_to(d)).start()
            scopy(j, 2, big(-d), mrec.at[j, 1], big_to(-d)).start()

        def s2():
            scopy(j, 1, mrec.at[j, 0], mrec.at[j, 0], partner).wait_recv()
            big(d)[...] = big(d)[...] + mrec[j, 0]
            scopy(j, 3, big(d), mrec.at[j, 2], big_to(d)).start()

        def s3():
            scopy(j, 2, mrec.at[j, 1], mrec.at[j, 1], partner).wait_recv()
            scopy(j, 3, mrec.at[j, 2], mrec.at[j, 2], partner).wait_recv()
            big(0)[...] = big(0)[...] + mrec[j, 1] + mrec[j, 2]
            scopy(j, 4, small(2), nrec.at[j, 0], small_to(d)).start()
            scopy(j, 5, small(-d), nrec.at[j, 1], small_to(-d)).start()

        def s4():
            scopy(j, 4, nrec.at[j, 0], nrec.at[j, 0], partner).wait_recv()
            small(d)[...] = small(d)[...] + nrec[j, 0]
            scopy(j, 6, small(d), nrec.at[j, 2], small_to(d)).start()

        def s5():
            scopy(j, 5, nrec.at[j, 1], nrec.at[j, 1], partner).wait_recv()
            scopy(j, 6, nrec.at[j, 2], nrec.at[j, 2], partner).wait_recv()
            val = part[j, c, x, y] + nrec[j, 1] + nrec[j, 2]
            out[:, pl.ds(pl.multiple_of(j * CW, CW), CW)] = val.astype(BF)

        def sends():
            scopy(j, 0, part.at[j, o], d2d.at[j], partner).wait_send()
            scopy(j, 1, big(2), mrec.at[j, 0], partner).wait_send()
            scopy(j, 2, big(-d), mrec.at[j, 1], partner).wait_send()
            scopy(j, 3, big(d), mrec.at[j, 2], partner).wait_send()
            scopy(j, 4, small(2), nrec.at[j, 0], partner).wait_send()
            scopy(j, 5, small(-d), nrec.at[j, 1], partner).wait_send()
            scopy(j, 6, small(d), nrec.at[j, 2], partner).wait_send()

        return s1, s2, s3, s4, s5, sends

    half = nch // 2

    def rs_step(t, carry):
        for hf in range(2):
            @pl.when(t < half)
            def _():
                down(2 * t + hf)

            for n_s in range(1, 6):
                hf2 = (hf + n_s) % 2
                i = t + (hf - n_s - hf2) // 2

                @pl.when((i >= 0) & (i < half))
                def _():
                    stages(i, hf2)[n_s - 1]()
        return carry

    lax.fori_loop(0, (nch + 6) // 2, rs_step, 0)

    def fin(i, carry):
        for hf in range(2):
            stages(i, hf)[5]()
        return carry

    lax.fori_loop(0, half, fin, 0)
    for k in range(nch):
        for kind in range(3):
            src = block(k, 0)
            rcopy(k, kind, src, src, partner).wait_send()
        for kind in range(3, 10):
            rcopy(k, kind, lines(k, 0, c), lines(k, 0, c), partner).wait_send()


def solution(mesh):
    ep_n, ny = mesh.shape["ep"], mesh.shape["tp"]
    nx = ep_n // 2
    row_spec = P(("dp", "ep", "tp"), None)

    def layer(tokens, expert_ids, gates, w_gate, w_up, w_down):
        rows, hid = tokens.shape
        ne, ff, _ = w_down.shape
        group = rows * ep_n * ny
        nch = hid // CW
        dims = (nx, ny, ne, ff, rows, hid)
        vm = pl.BlockSpec(memory_space=pltpu.VMEM)
        hbm = pl.BlockSpec(memory_space=pl.ANY)
        dma = pltpu.SemaphoreType.DMA
        line = ny * rows
        scratch = [
            pltpu.VMEM((nch, 2, nx, ny, rows, CW), BF),
            pltpu.VMEM((ep_n, 1, 2 * line), F32),
            pltpu.VMEM((ep_n * ny, 1, 2 * line), F32),
            pltpu.VMEM((group, group), BF),
            pltpu.VMEM((group, CW), BF),
            pltpu.VMEM((nch, ne, 2 * ff, CW), BF),
            pltpu.VMEM((ne // 2, 2 * ff, 2 * (group // ne)), F32),
            pltpu.VMEM((ff, group), BF),
            pltpu.VMEM((group, 128), F32),
            pltpu.VMEM((group, 128), F32),
            pltpu.VMEM((group, ne * ff), BF),
            pltpu.VMEM((WD_SLOTS, ne * ff, CW), BF),
            pltpu.VMEM((nch, 2, nx, ny, rows, CW), F32),
            pltpu.VMEM((nch, nx, ny, rows, CW), F32),
            pltpu.VMEM((nch, 3, nx, rows, CW), F32),
            pltpu.VMEM((nch, 3, rows, CW), F32),
            dma((nch, 10)), dma((nch, 10)), dma, dma, dma((nch, 2)), dma((WD_SLOTS,)),
            dma((nch, 7)), dma((nch, 7)),
        ]
        return pl.pallas_call(
            functools.partial(kernel, dims),
            out_shape=jax.ShapeDtypeStruct((rows, hid), BF),
            in_specs=[vm, vm, vm, hbm, hbm, hbm],
            out_specs=vm,
            scratch_shapes=scratch,
            compiler_params=pltpu.CompilerParams(collective_id=0, has_side_effects=True,
                                                 vmem_limit_bytes=67_043_328),
        )(tokens, expert_ids.T, gates.T, jnp.swapaxes(w_gate, 1, 2), jnp.swapaxes(w_up, 1, 2),
          w_down.reshape(ne * ff, hid))

    w_spec = P("ep", None, "tp")
    return jax.shard_map(layer, mesh=mesh, in_specs=(row_spec, row_spec, row_spec, w_spec, w_spec, P("ep", "tp", None)),
                         out_specs=row_spec, check_vma=False)
```

time: 239 us -> 107 us (0.45)
  the two profiles are of different devices: /device:TPU:97 before, /device:TPU:102 now
where the time goes in v1:
time: 107 us; the launch traced here: 106 us
  Pallas kernels  105 us (98%)
  local copies, waits for them, and re-layouts  1.57 us (1%)
    pallas_call x1, Pallas kernels, layer(): pl.pallas_call(functools.partial(kernel, dims), out_shape=jax.ShapeDtypeS...  105 us

profile of v1, /device:TPU:102, one launch (start us, length us, event | category | flops | bytes accessed | tf_op | source)
XLA Modules:
  0.0 106.4 jit_solution(11372306276143699870)
XLA Ops:
  0.0 104.8 %shard_map.64 = bf16[32,2048]{1,0:T(8,128)(2,1)} custom-call(bf16[32,2048]{1,0:T(8,128)(2,1)} %tok.1, s32[8,32]{1,0:T(8,128)} %bitcast.8, f32[8,32]{1,0:T(8,128)} %bitcast.9, bf16[16,192,2048]{2,1,0:T(8,128)(2,1)} %bitcast.5, bf16[16,192,2048]{2,1,0:T(8,128)(2,1)} %bitcast.6, bf16[3072,2048]{1,0:T(8,128)(2,1)} %bitcast.7), custom_call_target="tpu_custom_call" | custom-call | tf_op jit(solution)/shard_map/pallas_call | solution.py:411
  104.8 1.6 %copy.8 = bf16[32,2048]{1,0:T(8,128)(2,1)} copy(bf16[32,2048]{1,0:T(8,128)(2,1)} %shard_map.64) | data formatting | bytes 262144

commit v2 on v1

v2 whole, which is shorter than its diff:
```python
import functools

import jax
import jax.numpy as jnp
from jax import lax
from jax.experimental import pallas as pl
from jax.experimental.pallas import tpu as pltpu
from jax.sharding import PartitionSpec as P

MESH = pl.DeviceIdType.MESH
BF = jnp.bfloat16
F32 = jnp.float32
CW = 256
WD_SLOTS = 4
AG_LAGS = (0, 2, 4, 6, 7, 7)
PERM_AT = 4
RS_LAGS = (1, 3, 5, 7, 9)


def kernel(dims, tok, ids, gat, wg, wu, wd, out,
           xg, meta_src, meta, pmat, xs, wbuf, acc, h_t, lecol, gcol, hexp, wdbuf,
           part, d2d, mrec, nrec,
           ag_send, ag_recv, meta_send, meta_recv, w_sem, wd_sem, rs_send, rs_recv):
    nx, ny, ne, ff, rows, hid = dims
    nch = hid // CW
    group = 2 * nx * ny * rows
    plane = group // 2
    line = ny * rows
    load = group // ne
    ep_n = 2 * nx
    y = lax.axis_index("tp")
    ep = lax.axis_index("ep")
    x = ep // 2
    c = ep % 2
    o = 1 - c

    def dev(xx, yy, cc):
        return {"tp": yy, "ep": 2 * xx + cc}

    def xo(s):
        return lax.rem(x + s + 2 * nx, nx)

    def yo(s):
        return lax.rem(y + s + 2 * ny, ny)

    def w_copy(k, which):
        src = (wg, wu)[which]
        return pltpu.make_async_copy(src.at[:, :, pl.ds(pl.multiple_of(k * CW, CW) if not isinstance(k, int) else k * CW, CW)],
                                     wbuf.at[k, :, pl.ds(which * ff, ff), :], w_sem.at[k])

    def wd_copy(j):
        return pltpu.make_async_copy(wd.at[:, pl.ds(j * CW, CW)], wdbuf.at[j % WD_SLOTS], wd_sem.at[j % WD_SLOTS])

    barrier = pltpu.get_barrier_semaphore()
    n_dev = ep_n * ny
    me = y * ep_n + ep

    def greet(i, carry):
        flat = lax.rem(me + i, n_dev)
        pl.semaphore_signal(barrier, inc=1, device_id={"tp": flat // ep_n, "ep": lax.rem(flat, ep_n)},
                            device_id_type=MESH)
        return carry

    with jax.named_scope("greet"):
        lax.fori_loop(1, n_dev, greet, 0)

    with jax.named_scope("w_issue"):
        for k in range(nch):
            for which in range(2):
                w_copy(k, which).start()
        for j in range(WD_SLOTS):
            wd_copy(j).start()

    ids4 = jnp.concatenate([ids[...]] * ny, axis=1)
    gat4 = jnp.concatenate([gat[...]] * ny, axis=1)
    lane = lax.broadcasted_iota(jnp.int32, (1, line), 1)
    mine = (lane // rows) == y
    for p in range(ep_n):
        sel = (ids4 // ne) == p
        le = jnp.sum(jnp.where(sel, ids4 - p * ne, 0).astype(F32), axis=0, keepdims=True)
        ga = jnp.sum(jnp.where(sel, gat4, 0.0), axis=0, keepdims=True)
        meta_src[p, :, pl.ds(0, line)] = jnp.where(mine, le, 0.0)
        meta_src[p, :, pl.ds(line, line)] = jnp.where(mine, ga, 0.0)
    my_block = (c * nx + x) * ny + y
    meta[my_block] = meta_src[ep]
    for k in range(nch):
        xg[k, c, x, y] = tok[:, pl.ds(k * CW, CW)]

    acc[...] = jnp.zeros_like(acc)
    with jax.named_scope("barrier"):
        pl.semaphore_wait(barrier, n_dev - 1)

    def send_meta(i, carry):
        flat = lax.rem(me + i, n_dev)
        pe = lax.rem(flat, ep_n)
        pltpu.make_async_remote_copy(
            src_ref=meta_src.at[pe], dst_ref=meta.at[my_block], send_sem=meta_send, recv_sem=meta_recv,
            device_id={"tp": flat // ep_n, "ep": pe}, device_id_type=MESH).start()
        return carry

    lax.fori_loop(1, n_dev, send_meta, 0)

    partner = dev(x, y, o)

    def gather(i, hf):
        k = 2 * i + hf
        d = 1 - 2 * lax.rem(i, 2)

        def first_to(s):
            return dev(xo(s), y, c) if hf == 0 else dev(x, yo(s), c)

        def second_to(s):
            return dev(x, yo(s), c) if hf == 0 else dev(xo(s), y, c)

        def block(s):
            return xg.at[k, c, xo(s), y] if hf == 0 else xg.at[k, c, x, yo(s)]

        def lines(s, cc):
            return xg.at[k, cc, :, yo(s)] if hf == 0 else xg.at[k, cc, xo(s)]

        def rcopy(kind, src, dst, to):
            return pltpu.make_async_remote_copy(src_ref=src, dst_ref=dst, send_sem=ag_send,
                                                recv_sem=ag_recv.at[k, min(kind, 6) if isinstance(kind, int) else kind], device_id=to, device_id_type=MESH)

        def wait(kind, dst):
            rcopy(kind, dst, dst, partner).wait_recv()

        def a0():
            src = tok.at[:, pl.ds(pl.multiple_of(k * CW, CW), CW)]
            rcopy(0, src, block(0), first_to(1)).start()
            rcopy(1, src, block(0), first_to(-1)).start()

        def a1():
            back = jnp.where(d == 1, 0, 1)
            wait(back, block(-d))
            rcopy(2, block(-d), block(-d), first_to(d)).start()
            wait(1 - back, block(d))

        def a2():
            wait(2, block(2))
            rcopy(3, lines(0, c), lines(0, c), second_to(1)).start()
            rcopy(4, lines(0, c), lines(0, c), second_to(-1)).start()
            rcopy(6, lines(0, c), lines(0, c), partner).start()

        def a3():
            back = jnp.where(d == 1, 3, 4)
            wait(back, lines(-d, c))
            rcopy(5, lines(-d, c), lines(-d, c), second_to(d)).start()
            rcopy(7, lines(-d, c), lines(-d, c), partner).start()
            wait(7 - back, lines(d, c))
            rcopy(8, lines(d, c), lines(d, c), partner).start()

        def a4():
            wait(5, lines(2, c))
            rcopy(9, lines(2, c), lines(2, c), partner).start()

        def a5():
            wait(6, xg.at[k, o])

        return a0, a1, a2, a3, a4, a5

    n_grp = 2 * nx

    def build_perm():
        all_meta = meta.at[pl.ds(0, n_dev - 1)]
        pltpu.make_async_remote_copy(src_ref=all_meta, dst_ref=all_meta, send_sem=meta_send, recv_sem=meta_recv,
                                     device_id=partner, device_id_type=MESH).wait()
        les, gas = [], []
        for g in range(n_grp):
            row = meta[g * ny]
            for i in range(1, ny):
                row = row + meta[g * ny + i]
            les.append(row[:, :line])
            gas.append(row[:, line:])
        e_iota = lax.broadcasted_iota(jnp.int32, (ne, line), 0).astype(F32)
        hots = [jnp.where(e_iota == le, 1.0, 0.0) for le in les]
        r_i = lax.broadcasted_iota(jnp.int32, (line, line), 0)
        c_i = lax.broadcasted_iota(jnp.int32, (line, line), 1)
        upper = jnp.where(r_i < c_i, 1.0, 0.0).astype(BF)
        before = jnp.dot(jnp.concatenate(hots, axis=0).astype(BF), upper, preferred_element_type=F32)
        off = jnp.zeros((ne, 1), F32)
        s_iota = lax.broadcasted_iota(jnp.int32, (group, line), 0).astype(F32)
        for g in range(n_grp):
            pos = jnp.sum(hots[g] * (e_iota * load + off + before[g * ne:(g + 1) * ne]), axis=0, keepdims=True)
            off = off + jnp.sum(hots[g], axis=1, keepdims=True)
            pmat[:, pl.ds(g * line, line)] = jnp.where(s_iota == pos, 1.0, 0.0).astype(BF)
        le_t = jnp.concatenate(les, axis=0).T
        ga_t = jnp.concatenate(gas, axis=0).T
        for g in range(n_grp):
            lecol[pl.ds(g * line, line), :] = jnp.broadcast_to(le_t[:, g:g + 1], (line, 128)).astype(BF)
            gcol[pl.ds(g * line, line), :] = jnp.broadcast_to(ga_t[:, g:g + 1], (line, 128))

    half_lane = lax.broadcasted_iota(jnp.int32, (2 * ff, 2 * load), 1) < load

    def compute(k):
        xk = xg.at[k].reshape(group, CW)
        with jax.named_scope("perm"):
            for m in range(2):
                sl = pl.ds(m * (group // 2), group // 2)
                xs[sl, :] = jnp.dot(pmat[sl, :], xk[...], preferred_element_type=F32).astype(BF)
        pltpu.make_async_copy(wbuf.at[k], wbuf.at[k], w_sem.at[k]).wait()
        dn = (((1,), (1,)), ((), ()))
        with jax.named_scope("pairs"):
            for p in range(ne // 2):
                rhs = xs[pl.ds(p * 2 * load, 2 * load), :]
                r0 = lax.dot_general(wbuf[k, 2 * p], rhs, dn, preferred_element_type=F32)
                r1 = lax.dot_general(wbuf[k, 2 * p + 1], rhs, dn, preferred_element_type=F32)
                acc[p] = acc[p] + jnp.where(half_lane, r0, r1)

    half = nch // 2

    def each(fn):
        def go(i, carry):
            for hf in range(2):
                fn(i, hf)
            return carry
        lax.fori_loop(0, half, go, 0)

    def pipeline(stages, first, last):
        def go(t, carry):
            for hf in range(2):
                for lag, name, fn in stages:
                    hf2 = (hf + lag) % 2
                    i = t + (hf - lag - hf2) // 2

                    @pl.when((i >= 0) & (i < half))
                    def _():
                        with jax.named_scope(name):
                            fn(i, hf2)
            return carry
        lax.fori_loop(first // 2, last // 2, go, 0)

    with jax.named_scope("a0"):
        each(lambda i, hf: gather(i, hf)[0]())
    ag = [(lag, f"ag{n}", lambda i, hf, n=n: gather(i, hf)[n]()) for n, lag in enumerate(AG_LAGS[:5], 1)]
    ag.append((AG_LAGS[5], "compute", lambda i, hf: compute(2 * i + hf)))
    pipeline(ag, 0, PERM_AT)
    with jax.named_scope("build_perm"):
        build_perm()
    pipeline(ag, PERM_AT, (nch + max(AG_LAGS) + 1) // 2 * 2)

    with jax.named_scope("silu"):
        for p in range(ne // 2):
            a = acc[p, :ff, :]
            b = acc[p, ff:, :]
            h_t[:, pl.ds(p * 2 * load, 2 * load)] = (jax.nn.silu(a) * b).astype(BF)
    wide = 4 * ff

    def expand(cc):
        col_e = (lax.broadcasted_iota(jnp.int32, (line, wide), 1) // ff).astype(BF)
        ht = jnp.dot(h_t[...], pmat[:, pl.ds(pl.multiple_of(cc * plane, plane), plane)], preferred_element_type=F32)
        for g in range(plane // line):
            sl = pl.ds(pl.multiple_of(cc * plane + g * line, line), line)
            h = ht[:, g * line:(g + 1) * line].T.astype(BF)
            rep = jnp.concatenate([h] * 4, axis=1)
            le = jnp.concatenate([lecol[sl, :]] * (wide // 128), axis=1)
            for q in range(ne // 4):
                hexp[sl, pl.ds(q * wide, wide)] = jnp.where(col_e + BF(4 * q) == le, rep, BF(0))

    def scopy(j, kind, src, dst, to):
        return pltpu.make_async_remote_copy(src_ref=src, dst_ref=dst, send_sem=rs_send,
                                            recv_sem=rs_recv.at[j, kind], device_id=to, device_id_type=MESH)

    def down_half(j, slot, i):
        cc = jnp.where(i == 0, o, c)
        base = pl.multiple_of(cc * plane, plane)
        v = jnp.dot(hexp[pl.ds(base, plane), :], wdbuf[slot], preferred_element_type=F32)
        gt = gcol[pl.ds(base, plane), :]
        v = jnp.concatenate([v[:, q * 128:(q + 1) * 128] * gt for q in range(CW // 128)], axis=1)
        part[j, cc] = v.reshape(nx, ny, rows, CW)

        @pl.when(i == 0)
        def _():
            scopy(j, 0, part.at[j, o], d2d.at[j], partner).start()

    def down(j):
        slot = lax.rem(j, WD_SLOTS)
        pltpu.make_async_copy(wd.at[:, pl.ds(0, CW)], wdbuf.at[slot], wd_sem.at[slot]).wait()

        def one(i, carry):
            @pl.when(j == 0)
            def _():
                with jax.named_scope("expand"):
                    expand(jnp.where(i == 0, o, c))
            with jax.named_scope("half"):
                down_half(j, slot, i)
            return carry

        lax.fori_loop(0, 2, one, 0)

        @pl.when(j + WD_SLOTS < nch)
        def _():
            pltpu.make_async_copy(wd.at[:, pl.ds(pl.multiple_of((j + WD_SLOTS) * CW, CW), CW)],
                                  wdbuf.at[slot], wd_sem.at[slot]).start()

    def stages(i, hf):
        j = 2 * i + hf
        d = 1 - 2 * lax.rem(i, 2)

        def xd(s):
            return lax.rem(x + s + 2 * nx, nx)

        def yd(s):
            return lax.rem(y + s + 2 * ny, ny)

        def big(s):
            return part.at[j, c, :, yd(s)] if hf == 0 else part.at[j, c, xd(s)]

        def big_to(s):
            return dev(x, yd(s), c) if hf == 0 else dev(xd(s), y, c)

        def small(s):
            return part.at[j, c, xd(s), y] if hf == 0 else part.at[j, c, x, yd(s)]

        def small_to(s):
            return dev(xd(s), y, c) if hf == 0 else dev(x, yd(s), c)

        def s1():
            scopy(j, 0, d2d.at[j], d2d.at[j], partner).wait_recv()
            part[j, c] = part[j, c] + d2d[j]
            scopy(j, 1, big(2), mrec.at[j, 0], big_to(d)).start()
            scopy(j, 2, big(-d), mrec.at[j, 1], big_to(-d)).start()

        def s2():
            scopy(j, 1, mrec.at[j, 0], mrec.at[j, 0], partner).wait_recv()
            big(d)[...] = big(d)[...] + mrec[j, 0]
            scopy(j, 2, big(d), mrec.at[j, 2], big_to(d)).start()

        def s3():
            scopy(j, 2, mrec.at[j, pl.ds(1, 2)], mrec.at[j, pl.ds(1, 2)], partner).wait_recv()
            big(0)[...] = big(0)[...] + mrec[j, 1] + mrec[j, 2]
            scopy(j, 3, small(2), nrec.at[j, 0], small_to(d)).start()
            scopy(j, 4, small(-d), nrec.at[j, 1], small_to(-d)).start()

        def s4():
            scopy(j, 3, nrec.at[j, 0], nrec.at[j, 0], partner).wait_recv()
            small(d)[...] = small(d)[...] + nrec[j, 0]
            scopy(j, 4, small(d), nrec.at[j, 2], small_to(d)).start()

        def s5():
            scopy(j, 4, nrec.at[j, pl.ds(1, 2)], nrec.at[j, pl.ds(1, 2)], partner).wait_recv()
            val = part[j, c, x, y] + nrec[j, 1] + nrec[j, 2]
            out[:, pl.ds(pl.multiple_of(j * CW, CW), CW)] = val.astype(BF)

        return s1, s2, s3, s4, s5

    rs = [(0, "down", lambda i, hf: down(2 * i + hf))]
    rs += [(lag, f"rs{n}", lambda i, hf, n=n: stages(i, hf)[n - 1]()) for n, lag in enumerate(RS_LAGS, 1)]
    pipeline(rs, 0, (nch + max(RS_LAGS) + 1) // 2 * 2)
    with jax.named_scope("fin"):
        blocks = nch * (3 + 7 * nx)
        for buf, sem in ((xg, ag_send), (part, rs_send)):
            flat = buf.reshape(nch * 2 * nx * ny, rows, CW).at[pl.ds(0, blocks)]
            pltpu.make_async_remote_copy(src_ref=flat, dst_ref=flat, send_sem=sem, recv_sem=sem,
                                         device_id=partner, device_id_type=MESH).wait_send()


def solution(mesh):
    ep_n, ny = mesh.shape["ep"], mesh.shape["tp"]
    nx = ep_n // 2
    row_spec = P(("dp", "ep", "tp"), None)

    def layer(tokens, expert_ids, gates, w_gate, w_up, w_down):
        rows, hid = tokens.shape
        ne, ff, _ = w_down.shape
        group = rows * ep_n * ny
        nch = hid // CW
        dims = (nx, ny, ne, ff, rows, hid)
        vm = pl.BlockSpec(memory_space=pltpu.VMEM)
        hbm = pl.BlockSpec(memory_space=pl.ANY)
        dma = pltpu.SemaphoreType.DMA
        line = ny * rows
        scratch = [
            pltpu.VMEM((nch, 2, nx, ny, rows, CW), BF),
            pltpu.VMEM((ep_n, 1, 2 * line), F32),
            pltpu.VMEM((ep_n * ny, 1, 2 * line), F32),
            pltpu.VMEM((group, group), BF),
            pltpu.VMEM((group, CW), BF),
            pltpu.VMEM((nch, ne, 2 * ff, CW), BF),
            pltpu.VMEM((ne // 2, 2 * ff, 2 * (group // ne)), F32),
            pltpu.VMEM((ff, group), BF),
            pltpu.VMEM((group, 128), BF),
            pltpu.VMEM((group, 128), F32),
            pltpu.VMEM((group, ne * ff), BF),
            pltpu.VMEM((WD_SLOTS, ne * ff, CW), BF),
            pltpu.VMEM((nch, 2, nx, ny, rows, CW), F32),
            pltpu.VMEM((nch, nx, ny, rows, CW), F32),
            pltpu.VMEM((nch, 3, nx, rows, CW), F32),
            pltpu.VMEM((nch, 3, rows, CW), F32),
            dma, dma((nch, 7)), dma, dma, dma((nch,)), dma((WD_SLOTS,)),
            dma, dma((nch, 5)),
        ]
        return pl.pallas_call(
            functools.partial(kernel, dims),
            out_shape=jax.ShapeDtypeStruct((rows, hid), BF),
            in_specs=[vm, vm, vm, hbm, hbm, hbm],
            out_specs=vm,
            scratch_shapes=scratch,
            compiler_params=pltpu.CompilerParams(collective_id=0, has_side_effects=True,
                                                 vmem_limit_bytes=67_043_328),
        )(tokens, expert_ids.T, gates.T, jnp.swapaxes(w_gate, 1, 2), jnp.swapaxes(w_up, 1, 2),
          w_down.reshape(ne * ff, hid))

    w_spec = P("ep", None, "tp")
    return jax.shard_map(layer, mesh=mesh, in_specs=(row_spec, row_spec, row_spec, w_spec, w_spec, P("ep", "tp", None)),
                         out_specs=row_spec, check_vma=False)
```

time: 107 us -> 81.9 us (0.77)
  the two profiles are of different devices: /device:TPU:102 before, /device:TPU:96 now
where the time goes in v2:
time: 81.9 us; the launch traced here: 81.8 us
  Pallas kernels  80.2 us (98%)
  local copies, waits for them, and re-layouts  1.57 us (2%)
    pallas_call x1, Pallas kernels, layer(): pl.pallas_call(functools.partial(kernel, dims), out_shape=jax.ShapeDtypeS...  80.2 us

profile of v2, /device:TPU:96, one launch (start us, length us, event | category | flops | bytes accessed | tf_op | source)
XLA Modules:
  0.0 81.8 jit_solution(3910571073796714302)
XLA Ops:
  0.0 80.2 %shard_map.64 = bf16[32,2048]{1,0:T(8,128)(2,1)} custom-call(bf16[32,2048]{1,0:T(8,128)(2,1)} %tok.1, s32[8,32]{1,0:T(8,128)} %bitcast.8, f32[8,32]{1,0:T(8,128)} %bitcast.9, bf16[16,192,2048]{2,1,0:T(8,128)(2,1)} %bitcast.5, bf16[16,192,2048]{2,1,0:T(8,128)(2,1)} %bitcast.6, bf16[3072,2048]{1,0:T(8,128)(2,1)} %bitcast.7), custom_call_target="tpu_custom_call" | custom-call | tf_op jit(solution)/shard_map/pallas_call | solution.py:393
  80.2 1.6 %copy.8 = bf16[32,2048]{1,0:T(8,128)(2,1)} copy(bf16[32,2048]{1,0:T(8,128)(2,1)} %shard_map.64) | data formatting | bytes 262144

commit v3 on v2

v3 whole, which is shorter than its diff:
```python
import functools

import jax
import jax.numpy as jnp
from jax import lax
from jax.experimental import pallas as pl
from jax.experimental.pallas import tpu as pltpu
from jax.sharding import PartitionSpec as P

MESH = pl.DeviceIdType.MESH
BF = jnp.bfloat16
F32 = jnp.float32
CW = 256
WD_SLOTS = 3
N_DIRECT = 3
DIRECT = 0
FILL = ("0.0", "0.1", "0.2", "0.3", "0.4", "0.5", "0.6", "0.7", "m1", "1.0", "1.1", "1.2", "1.3", "m2", "2.0", "2.1",
        "1.4", "1.5", "b", "2.2", "2.3", "3.0", "3.1", "1.6", "1.7")
RS_LAGS = (1, 3, 5, 8, 10)
M2_LATE = 8


def kernel(dims, tok_hbm, ids_hbm, gat_hbm, wg, wu, wd, out,
           tok, ids, gat, in_sem, xg, meta_src, meta, pmat, xs, wbuf, acc, h_t, lecol, gcol, hexp, wdbuf,
           part, d2d, mrec, nrec,
           ag_send, ag_recv, meta_send, meta_recv, w_sem, wd_sem, rs_send, rs_recv):
    nx, ny, ne, ff, rows, hid = dims
    nch = hid // CW
    group = 2 * nx * ny * rows
    plane = group // 2
    line = ny * rows
    load = group // ne
    ep_n = 2 * nx
    y = lax.axis_index("tp")
    ep = lax.axis_index("ep")
    x = ep // 2
    c = ep % 2
    o = 1 - c

    def dev(xx, yy, cc):
        return {"tp": yy, "ep": 2 * xx + cc}

    def xo(s):
        return lax.rem(x + s + 2 * nx, nx)

    def yo(s):
        return lax.rem(y + s + 2 * ny, ny)

    def w_copy(k, which):
        src = (wg, wu)[which]
        return pltpu.make_async_copy(src.at[:, :, pl.ds(pl.multiple_of(k * CW, CW) if not isinstance(k, int) else k * CW, CW)],
                                     wbuf.at[k, :, pl.ds(which * ff, ff), :], w_sem.at[k])

    def wd_copy(j):
        return pltpu.make_async_copy(wd.at[:, pl.ds(j * CW, CW)], wdbuf.at[j % WD_SLOTS], wd_sem.at[j % WD_SLOTS])

    barrier = pltpu.get_barrier_semaphore()
    peers = [dev(xo(i), y, c) for i in range(1, nx)] + [dev(x, yo(i), c) for i in range(1, ny)] + [dev(x, y, o)]
    for peer in peers:
        pl.semaphore_signal(barrier, inc=1, device_id=peer, device_id_type=MESH)

    own = [pltpu.make_async_copy(src, dst, in_sem.at[n])
           for n, (src, dst) in enumerate(((ids_hbm, ids), (gat_hbm, gat), (tok_hbm, tok)))]
    for copy in own:
        copy.start()
    with jax.named_scope("w_issue"):
        for k in range(nch):
            for which in range(2):
                w_copy(k, which).start()
        for j in range(WD_SLOTS):
            wd_copy(j).start()

    own[0].wait()
    own[1].wait()
    ids4 = jnp.concatenate([ids[...]] * ny, axis=1)
    gat4 = jnp.concatenate([gat[...]] * ny, axis=1)
    lane = lax.broadcasted_iota(jnp.int32, (1, line), 1)
    mine = (lane // rows) == y
    for p in range(ep_n):
        sel = (ids4 // ne) == p
        le = jnp.sum(jnp.where(sel, ids4 - p * ne, 0).astype(F32), axis=0, keepdims=True)
        ga = jnp.sum(jnp.where(sel, gat4, 0.0), axis=0, keepdims=True)
        meta_src[p, :, pl.ds(0, line)] = jnp.where(mine, le, 0.0)
        meta_src[p, :, pl.ds(line, line)] = jnp.where(mine, ga, 0.0)
    for e2 in range(2):
        meta[c, x, y, e2] = meta_src[2 * x + e2]
    own[2].wait()
    for k in range(nch):
        xg[k, c, x, y] = tok[:, pl.ds(k * CW, CW)]

    acc[...] = jnp.zeros_like(acc)
    with jax.named_scope("barrier"):
        pl.semaphore_wait(barrier, len(peers))

    def mcopy(n, src, dst, to):
        return pltpu.make_async_remote_copy(src_ref=src, dst_ref=dst, send_sem=meta_send.at[n], recv_sem=meta_recv.at[n],
                                            device_id=to, device_id_type=MESH)

    def meta0():
        for i in range(1, nx):
            mcopy(0, meta_src.at[pl.ds(2 * xo(i), 2)], meta.at[c, x, y], dev(xo(i), y, c)).start()

    def meta1():
        whole = meta_src.at[pl.ds(0, 2 * (nx - 1))]
        mcopy(0, whole, whole, dev(x, y, o)).wait()
        for i in range(1, ny):
            mcopy(1, meta.at[c, :, y], meta.at[c, :, y], dev(x, yo(i), c)).start()

    def meta2():
        whole = meta.at[c, :, pl.ds(0, ny - 1)]
        mcopy(1, whole, whole, dev(x, y, o)).wait()
        mcopy(2, meta.at[c], meta.at[c], dev(x, y, o)).start()

    partner = dev(x, y, o)
    hw = CW // 2

    def gather(i, hf, direct=False):
        k = 2 * i + hf

        def first_to(s):
            return dev(xo(s), y, c) if hf == 0 else dev(x, yo(s), c)

        def second_to(s):
            return dev(x, yo(s), c) if hf == 0 else dev(xo(s), y, c)

        def block(s):
            return xg.at[k, c, xo(s), y] if hf == 0 else xg.at[k, c, x, yo(s)]

        def lines(s, cc, sub=slice(None)):
            return xg.at[k, cc, sub, yo(s)] if hf == 0 else xg.at[k, cc, xo(s), sub]

        def rcopy(kind, ref, to, src=None):
            return pltpu.make_async_remote_copy(src_ref=ref if src is None else src, dst_ref=ref, send_sem=ag_send,
                                                recv_sem=ag_recv.at[k, kind], device_id=to, device_id_type=MESH)

        def a0():
            src = tok.at[:, pl.ds(pl.multiple_of(k * CW, CW), CW)]
            for s in (1, -1, 2):
                rcopy(0, block(0), first_to(s), src).start()

        def a1():
            rcopy(0, xg.at[k, c, 0, pl.ds(0, 3)], partner).wait_recv()
            rcopy(1, lines(0, c), second_to(1)).start()
            rcopy(2, lines(0, c), second_to(-1)).start()
            if direct:
                rcopy(3, lines(0, c), second_to(2)).start()
            rcopy(4, lines(0, c), partner).start()

        def a2():
            for n, s in ((1, -1), (2, 1)):
                rcopy(n, lines(s, c), partner).wait_recv()
                if not direct:
                    rcopy(3, lines(s, c, pl.ds((n - 1) * (nx // 2), nx // 2)), second_to(-s)).start()
                rcopy(4, lines(s, c), partner).start()

        def a3():
            rcopy(3, lines(2, c), partner).wait_recv()
            rcopy(4, lines(2, c), partner).start()

        def a4():
            rcopy(4, xg.at[k, o], partner).wait_recv()

        return a0, a1, a2, a3, a4

    n_grp = 2 * nx

    def build_perm():
        mcopy(2, meta.at[c], meta.at[o], dev(x, y, o)).wait()
        les, gas = [], []
        for g in range(n_grp):
            row = meta[g // nx, g % nx, 0, c]
            for i in range(1, ny):
                row = row + meta[g // nx, g % nx, i, c]
            les.append(row[:, :line])
            gas.append(row[:, line:])
        e_iota = lax.broadcasted_iota(jnp.int32, (ne, line), 0).astype(F32)
        hots = [jnp.where(e_iota == le, 1.0, 0.0) for le in les]
        r_i = lax.broadcasted_iota(jnp.int32, (line, line), 0)
        c_i = lax.broadcasted_iota(jnp.int32, (line, line), 1)
        upper = jnp.where(r_i < c_i, 1.0, 0.0).astype(BF)
        before = jnp.dot(jnp.concatenate(hots, axis=0).astype(BF), upper, preferred_element_type=F32)
        off = jnp.zeros((ne, 1), F32)
        s_iota = lax.broadcasted_iota(jnp.int32, (group, line), 0).astype(F32)
        for g in range(n_grp):
            pos = jnp.sum(hots[g] * (e_iota * load + off + before[g * ne:(g + 1) * ne]), axis=0, keepdims=True)
            off = off + jnp.sum(hots[g], axis=1, keepdims=True)
            pmat[:, pl.ds(g * line, line)] = jnp.where(s_iota == pos, 1.0, 0.0).astype(BF)
        le_t = jnp.concatenate(les, axis=0).T
        ga_t = jnp.concatenate(gas, axis=0).T
        for g in range(n_grp):
            lecol[pl.ds(g * line, line), :] = jnp.broadcast_to(le_t[:, g:g + 1], (line, 128)).astype(BF)
            gcol[pl.ds(g * line, line), :] = jnp.broadcast_to(ga_t[:, g:g + 1], (line, 128))

    half_lane = lax.broadcasted_iota(jnp.int32, (2 * ff, 2 * load), 1) < load

    def compute(k):
        xk = xg.at[k].reshape(group, CW)
        with jax.named_scope("perm"):
            for m in range(2):
                sl = pl.ds(m * (group // 2), group // 2)
                xs[sl, :] = jnp.dot(pmat[sl, :], xk[...], preferred_element_type=F32).astype(BF)
        pltpu.make_async_copy(wbuf.at[k], wbuf.at[k], w_sem.at[k]).wait()
        dn = (((1,), (1,)), ((), ()))
        with jax.named_scope("pairs"):
            for p in range(ne // 2):
                rhs = xs[pl.ds(p * 2 * load, 2 * load), :]
                both = wbuf[k, pl.ds(2 * p, 2)].reshape(4 * ff, CW)
                r = lax.dot_general(both, rhs, dn, preferred_element_type=F32)
                acc[p] = acc[p] + jnp.where(half_lane, r[:2 * ff], r[2 * ff:])

    half = nch // 2

    meta0()
    done = [0] * 5
    for event in FILL:
        with jax.named_scope(event):
            if event in ("m1", "m2", "b"):
                {"m1": meta1, "m2": meta2, "b": build_perm}[event]()
            else:
                n, k = (int(v) for v in event.split("."))
                gather(k // 2, k % 2, k < DIRECT)[n]()
                done[n] = k + 1
    assert done[0] == nch

    def steady(i, carry):
        for hf in range(2):
            with jax.named_scope("ag4"):
                gather(i, hf)[4]()
            with jax.named_scope("compute"):
                compute(2 * i + hf)
            for n in range(1, 4):
                hf2 = (hf + done[n]) % 2
                ii = i + (hf + done[n] - hf2) // 2

                @pl.when(ii < half)
                def _():
                    with jax.named_scope(f"ag{n}"):
                        gather(ii, hf2)[n]()
        return carry

    lax.fori_loop(0, half, steady, 0)

    with jax.named_scope("silu"):
        for p in range(ne // 2):
            a = acc[p, :ff, :]
            b = acc[p, ff:, :]
            h_t[:, pl.ds(p * 2 * load, 2 * load)] = (jax.nn.silu(a) * b).astype(BF)
    wide = 4 * ff

    def expand(cc):
        col_e = (lax.broadcasted_iota(jnp.int32, (line, wide), 1) // ff).astype(BF)
        ht = jnp.dot(h_t[...], pmat[:, pl.ds(pl.multiple_of(cc * plane, plane), plane)], preferred_element_type=F32)
        for g in range(plane // line):
            sl = pl.ds(pl.multiple_of(cc * plane + g * line, line), line)
            h = ht[:, g * line:(g + 1) * line].T.astype(BF)
            rep = jnp.concatenate([h] * 4, axis=1)
            le = jnp.concatenate([lecol[sl, :]] * (wide // 128), axis=1)
            for q in range(ne // 4):
                hexp[sl, pl.ds(q * wide, wide)] = jnp.where(col_e + BF(4 * q) == le, rep, BF(0))

    def scopy(j, kind, src, dst, to):
        return pltpu.make_async_remote_copy(src_ref=src, dst_ref=dst, send_sem=rs_send,
                                            recv_sem=rs_recv.at[j, kind], device_id=to, device_id_type=MESH)

    def down_half(j, cc):
        base = pl.multiple_of(cc * plane, plane)

        @pl.when(j == 0)
        def _():
            with jax.named_scope("expand"):
                expand(cc)

        with jax.named_scope("half"):
            v = jnp.dot(hexp[pl.ds(base, plane), :], wdbuf[lax.rem(j, WD_SLOTS)], preferred_element_type=F32)
            gt = gcol[pl.ds(base, plane), :]
            for h in range(2):
                part[j, cc, h] = (v[:, h * hw:(h + 1) * hw] * gt).reshape(nx, ny, rows, hw)

    def wd_next(j):
        slot = lax.rem(j, WD_SLOTS)
        return pltpu.make_async_copy(wd.at[:, pl.ds(pl.multiple_of(j * CW, CW), CW)], wdbuf.at[slot], wd_sem.at[slot])

    def stages(j):
        ways = ((0, 1), (1, -1))
        q_rows = rows // 2

        def big(h, s, sub=slice(None)):
            return part.at[j, c, h, sub, yo(s)] if h == 0 else part.at[j, c, h, xo(s), sub]

        def small(h, s, sub=slice(None)):
            return part.at[j, c, h, xo(s), y, sub] if h == 0 else part.at[j, c, h, x, yo(s), sub]

        def to(along_y, s):
            return dev(x, yo(s), c) if along_y else dev(xo(s), y, c)

        def direct(part_of, rec, n, first, sem):
            for h in range(2):
                for q, s in ways:
                    sub = pl.ds((1 - q) * n, n)
                    scopy(j, sem + 1, part_of(h, s, sub), rec.at[j, h, 1 + q, sub], to((h == 0) == first, s)).start()

        def begin(part_of, rec, n, first, sem):
            for h in range(2):
                for q, s in ways:
                    sub = pl.ds(q * n, n)
                    scopy(j, sem, part_of(h, 2, sub), rec.at[j, h, 0, sub], to((h == 0) == first, s)).start()
            pl.when(j < M2_LATE)(lambda: direct(part_of, rec, n, first, sem))

        def go_on(part_of, rec, n, first, sem):
            scopy(j, sem, rec.at[j, :, 0], rec.at[j, :, 0], partner).wait_recv()
            for h in range(2):
                for q, s in ways:
                    sub = pl.ds(q * n, n)
                    mine = part_of(h, s, sub)
                    mine[...] = mine[...] + rec[j, h, 0, sub]
                    scopy(j, sem + 1, mine, rec.at[j, h, 1 + q, sub], to((h == 0) == first, s)).start()
            pl.when(j >= M2_LATE)(lambda: direct(part_of, rec, n, first, sem))

        def s1():
            scopy(j, 0, d2d.at[j], d2d.at[j], partner).wait_recv()
            part[j, c] = part[j, c] + d2d[j]
            begin(big, mrec, nx // 2, True, 1)

        def s2():
            go_on(big, mrec, nx // 2, True, 1)

        def s3():
            rest = mrec.at[j, :, pl.ds(1, 2)]
            scopy(j, 2, rest, rest, partner).wait_recv()
            for h in range(2):
                mine = big(h, 0)
                mine[...] = mine[...] + mrec[j, h, 1] + mrec[j, h, 2]

            @pl.when(j < nch - N_DIRECT)
            def _():
                begin(small, nrec, q_rows, False, 3)

            @pl.when(j >= nch - N_DIRECT)
            def _():
                for h in range(2):
                    for slot, s in enumerate((2, 1, -1)):
                        scopy(j, 4, small(h, s), nrec.at[j, h, slot], to(h == 1, s)).start()

        def s4():
            @pl.when(j < nch - N_DIRECT)
            def _():
                go_on(small, nrec, q_rows, False, 3)

        def s5():
            def finish(slots):
                rest = nrec.at[j, :, pl.ds(3 - slots, slots)]
                scopy(j, 4, rest, rest, partner).wait_recv()
                for h in range(2):
                    val = part[j, c, h, x, y]
                    for slot in range(3 - slots, 3):
                        val = val + nrec[j, h, slot]
                    out[:, pl.ds(pl.multiple_of(j * CW + h * hw, hw), hw)] = val.astype(BF)

            pl.when(j < nch - N_DIRECT)(lambda: finish(2))
            pl.when(j >= nch - N_DIRECT)(lambda: finish(3))

        return s1, s2, s3, s4, s5

    def rs_step(u, carry):
        @pl.when(u < nch)
        def _():
            wd_next(u).wait()
            down_half(u, o)
            scopy(u, 0, part.at[u, o], d2d.at[u], partner).start()

        @pl.when((u >= 2) & (u <= nch))
        def _():
            with jax.named_scope("rs1"):
                stages(u - 1)[0]()

        @pl.when(u < nch)
        def _():
            down_half(u, c)

        @pl.when(u < nch - WD_SLOTS)
        def _():
            wd_next(u + WD_SLOTS).start()

        @pl.when(u == 0)
        def _():
            with jax.named_scope("rs1"):
                stages(0)[0]()

        for n, lag in enumerate(RS_LAGS[1:], 1):
            j = u - lag

            @pl.when((j >= 0) & (j < nch))
            def _():
                with jax.named_scope(f"rs{n + 1}"):
                    stages(j)[n]()
        return carry

    lax.fori_loop(0, nch + max(RS_LAGS), rs_step, 0)
    with jax.named_scope("fin"):
        blocks = nch * (3 + 7 * nx)
        for buf, sem, n in ((xg, ag_send, 1), (part, rs_send, 2)):
            flat = buf.reshape(nch * 2 * n * nx * ny, rows, CW // n).at[pl.ds(0, blocks * n)]
            pltpu.make_async_remote_copy(src_ref=flat, dst_ref=flat, send_sem=sem, recv_sem=sem,
                                         device_id=partner, device_id_type=MESH).wait_send()


def solution(mesh):
    ep_n, ny = mesh.shape["ep"], mesh.shape["tp"]
    nx = ep_n // 2
    row_spec = P(("dp", "ep", "tp"), None)

    def layer(tokens, expert_ids, gates, w_gate, w_up, w_down):
        rows, hid = tokens.shape
        ne, ff, _ = w_down.shape
        group = rows * ep_n * ny
        nch = hid // CW
        dims = (nx, ny, ne, ff, rows, hid)
        vm = pl.BlockSpec(memory_space=pltpu.VMEM)
        hbm = pl.BlockSpec(memory_space=pl.ANY)
        dma = pltpu.SemaphoreType.DMA
        line = ny * rows
        scratch = [
            pltpu.VMEM((rows, hid), BF),
            pltpu.VMEM(expert_ids.shape[::-1], jnp.int32),
            pltpu.VMEM(gates.shape[::-1], F32),
            pltpu.SemaphoreType.DMA((3,)),
            pltpu.VMEM((nch, 2, nx, ny, rows, CW), BF),
            pltpu.VMEM((ep_n, 1, 2 * line), F32),
            pltpu.VMEM((2, nx, ny, 2, 1, 2 * line), F32),
            pltpu.VMEM((group, group), BF),
            pltpu.VMEM((group, CW), BF),
            pltpu.VMEM((nch, ne, 2 * ff, CW), BF),
            pltpu.VMEM((ne // 2, 2 * ff, 2 * (group // ne)), F32),
            pltpu.VMEM((ff, group), BF),
            pltpu.VMEM((group, 128), BF),
            pltpu.VMEM((group, 128), F32),
            pltpu.VMEM((group, ne * ff), BF),
            pltpu.VMEM((WD_SLOTS, ne * ff, CW), BF),
            pltpu.VMEM((nch, 2, 2, nx, ny, rows, CW // 2), F32),
            pltpu.VMEM((nch, 2, nx, ny, rows, CW // 2), F32),
            pltpu.VMEM((nch, 2, 3, nx, rows, CW // 2), F32),
            pltpu.VMEM((nch, 2, 3, rows, CW // 2), F32),
            dma, dma((nch, 5)), dma((3,)), dma((3,)), dma((nch,)), dma((WD_SLOTS,)),
            dma, dma((nch, 5)),
        ]
        return pl.pallas_call(
            functools.partial(kernel, dims),
            out_shape=pltpu.VMEM((rows, hid), BF),
            in_specs=[hbm] * 6,
            out_specs=vm,
            scratch_shapes=scratch,
            compiler_params=pltpu.CompilerParams(collective_id=0, has_side_effects=True,
                                                 vmem_limit_bytes=66_000_000),
        )(tokens, expert_ids.T, gates.T, jnp.swapaxes(w_gate, 1, 2), jnp.swapaxes(w_up, 1, 2),
          w_down.reshape(ne * ff, hid))

    w_spec = P("ep", None, "tp")
    return jax.shard_map(layer, mesh=mesh, in_specs=(row_spec, row_spec, row_spec, w_spec, w_spec, P("ep", "tp", None)),
                         out_specs=row_spec, check_vma=False)
```

time: 81.9 us -> 67.9 us (0.83)
  the two profiles are of different devices: /device:TPU:96 before, /device:TPU:97 now
where the time goes in v3:
time: 67.9 us; the launch traced here: 67.8 us
  Pallas kernels  67.2 us (99%)
    pallas_call x1, Pallas kernels, layer(): pl.pallas_call(functools.partial(kernel, dims), out_shape=pltpu.VMEM((row...  67.2 us

profile of v3, /device:TPU:97, one launch (start us, length us, event | category | flops | bytes accessed | tf_op | source)
XLA Modules:
  0.0 67.8 jit_solution(11670204042344314901)
XLA Ops:
  0.0 67.2 %shard_map.64 = bf16[32,2048]{1,0:T(8,128)(2,1)S(1)} custom-call(bf16[32,2048]{1,0:T(8,128)(2,1)} %tok_hbm.1, s32[8,32]{1,0:T(8,128)} %bitcast.8, f32[8,32]{1,0:T(8,128)} %bitcast.9, bf16[16,192,2048]{2,1,0:T(8,128)(2,1)} %bitcast.5, bf16[16,192,2048]{2,1,0:T(8,128)(2,1)} %bitcast.6, bf16[3072,2048]{1,0:T(8,128)(2,1)} %bitcast.7), custom_call_target="tpu_custom_call" | custom-call | tf_op jit(solution)/shard_map/pallas_call | solution.py:446
  67.2 0.7 copy.8

commit v4 on v3

--- a/solution.py
+++ b/solution.py
@@ -14,8 +14,8 @@
 WD_SLOTS = 3
 N_DIRECT = 3
 DIRECT = 0
-FILL = ("0.0", "0.1", "0.2", "0.3", "0.4", "0.5", "0.6", "0.7", "m1", "1.0", "1.1", "1.2", "1.3", "m2", "2.0", "2.1",
-        "1.4", "1.5", "b", "2.2", "2.3", "3.0", "3.1", "1.6", "1.7")
+FILL = ("m0", "0.0", "0.1", "0.2", "0.3", "0.4", "0.5", "0.6", "0.7", "m1", "1.0", "1.1", "1.2", "1.3", "m2", "2.0",
+        "2.1", "1.4", "1.5", "b", "2.2", "2.3", "3.0", "3.1", "1.6", "1.7")
 RS_LAGS = (1, 3, 5, 8, 10)
 M2_LATE = 8
 
@@ -194,12 +194,12 @@
     half_lane = lax.broadcasted_iota(jnp.int32, (2 * ff, 2 * load), 1) < load
 
     def compute(k):
+        pltpu.make_async_copy(wbuf.at[k], wbuf.at[k], w_sem.at[k]).wait()
         xk = xg.at[k].reshape(group, CW)
         with jax.named_scope("perm"):
-            for m in range(2):
-                sl = pl.ds(m * (group // 2), group // 2)
+            for m in range(4):
+                sl = pl.ds(m * (group // 4), group // 4)
                 xs[sl, :] = jnp.dot(pmat[sl, :], xk[...], preferred_element_type=F32).astype(BF)
-        pltpu.make_async_copy(wbuf.at[k], wbuf.at[k], w_sem.at[k]).wait()
         dn = (((1,), (1,)), ((), ()))
         with jax.named_scope("pairs"):
             for p in range(ne // 2):
@@ -210,12 +210,11 @@
 
     half = nch // 2
 
-    meta0()
     done = [0] * 5
     for event in FILL:
         with jax.named_scope(event):
-            if event in ("m1", "m2", "b"):
-                {"m1": meta1, "m2": meta2, "b": build_perm}[event]()
+            if event in ("m0", "m1", "m2", "b"):
+                {"m0": meta0, "m1": meta1, "m2": meta2, "b": build_perm}[event]()
             else:
                 n, k = (int(v) for v in event.split("."))
                 gather(k // 2, k % 2, k < DIRECT)[n]()
@@ -271,10 +270,13 @@
                 expand(cc)
 
         with jax.named_scope("half"):
-            v = jnp.dot(hexp[pl.ds(base, plane), :], wdbuf[lax.rem(j, WD_SLOTS)], preferred_element_type=F32)
-            gt = gcol[pl.ds(base, plane), :]
-            for h in range(2):
-                part[j, cc, h] = (v[:, h * hw:(h + 1) * hw] * gt).reshape(nx, ny, rows, hw)
+            n = plane // 2
+            for m in range(2):
+                sl = pl.ds(pl.multiple_of(base + m * n, n), n)
+                v = jnp.dot(hexp[sl, :], wdbuf[lax.rem(j, WD_SLOTS)], preferred_element_type=F32)
+                for h in range(2):
+                    part[j, cc, h, pl.ds(m * (nx // 2), nx // 2)] = (
+                        v[:, h * hw:(h + 1) * hw] * gcol[sl, :]).reshape(nx // 2, ny, rows, hw)
 
     def wd_next(j):
         slot = lax.rem(j, WD_SLOTS)

time: 67.9 us -> 66.7 us (0.982)
  Pallas kernels: 67.2 us -> 66 us
    pallas_call x1, Pallas kernels: 67.2 us -> 66 us  [layer(): pl.pallas_call(functools.partial(kernel, dims), out_shape=pltpu.VMEM((row...]
where the time goes in v4:
time: 66.7 us; the launch traced here: 66.6 us
  Pallas kernels  66 us (99%)
    pallas_call x1, Pallas kernels, layer(): pl.pallas_call(functools.partial(kernel, dims), out_shape=pltpu.VMEM((row...  66 us

profile of v4, /device:TPU:97, one launch (start us, length us, event | category | flops | bytes accessed | tf_op | source)
XLA Modules:
  0.0 66.6 jit_solution(17620182623041611258)
XLA Ops:
  0.0 66.0 %shard_map.64 = bf16[32,2048]{1,0:T(8,128)(2,1)S(1)} custom-call(bf16[32,2048]{1,0:T(8,128)(2,1)} %tok_hbm.1, s32[8,32]{1,0:T(8,128)} %bitcast.8, f32[8,32]{1,0:T(8,128)} %bitcast.9, bf16[16,192,2048]{2,1,0:T(8,128)(2,1)} %bitcast.5, bf16[16,192,2048]{2,1,0:T(8,128)(2,1)} %bitcast.6, bf16[3072,2048]{1,0:T(8,128)(2,1)} %bitcast.7), custom_call_target="tpu_custom_call" | custom-call | tf_op jit(solution)/shard_map/pallas_call | solution.py:448
  66.0 0.7 copy.8
